TPU v7x, 256 devices: a whole 4x4x8 slice. The times are simulated.
256 devices in a mesh: row: 4 (over z_hi, core), col: 64 (over x, y, z_lo).
Axes of the slice: x: 4, y: 4, z: 8 (z_hi: 2, z_lo: 4; z = z_hi * 4 + z_lo), core: 2. Of those that a mesh axis runs over, the one named last changes fastest.
Arguments:
- pre_act: bfloat16 [24576, 4096], P('col'), may hold values from -16 to 16
- grad_out: bfloat16 [24576, 4096], P('col', 'row'), may hold values from -6 to 6
- w_down: bfloat16 [4096, 4096], P('col', 'row'), may hold values from -0.09375 to 0.09375
Outputs:
- w_grad: float32 [4096, 4096], P('col', 'row')
- grad_pre: bfloat16 [24576, 4096], P('col', 'row')
All inputs are finite; a program needn't handle non-finite values.
Results may differ from a plain program's by a relative error of at most 0.0095.
Values may be sent and summed in bfloat16 or wider, within the bound.
A program may use at most 128 MiB of HBM per device.

v0:
```python
import jax
import jax.numpy as jnp
from jax import lax
from jax.sharding import Mesh
from jax.sharding import PartitionSpec as P

COL = ("col_0", "col_1", "col_2")


def summed_rows(subtotal, axes):
    for axis in axes:
        subtotal = lax.psum_scatter(subtotal, axis, scatter_dimension=0, tiled=True)
    return subtotal


def per_device(pre_act, grad_out, w_down):
    hidden = jnp.maximum(pre_act, jnp.zeros((), jnp.bfloat16))
    col_count = lax.axis_size(COL)
    row_count = lax.axis_size("row")
    scale = 1.0 / jnp.sqrt(jnp.float32(hidden.shape[0] * col_count))
    quarter = hidden.shape[1] // row_count
    partial_sum = lax.dot_general(
        grad_out,
        lax.all_gather(w_down, COL, axis=0, tiled=True),
        (((1,), (1,)), ((), ())),
        preferred_element_type=jnp.float32,
    )
    term = lax.dot_general(
        hidden, grad_out, (((0,), (0,)), ((), ())), preferred_element_type=jnp.float32
    )
    w_grad = summed_rows(term * scale, COL)
    own_sum = lax.psum_scatter(
        partial_sum.astype(jnp.bfloat16), "row", scatter_dimension=1, tiled=True
    ).astype(jnp.float32)
    offset_pre = lax.axis_index("row") * quarter
    own_pre = lax.dynamic_slice_in_dim(pre_act, offset_pre, quarter, 1)
    grad_pre = jnp.where(own_pre > 0, own_sum, jnp.zeros((), jnp.float32)).astype(jnp.bfloat16)
    return (w_grad, grad_pre)


def solution(mesh):
    torus = Mesh(
        mesh.devices.reshape(mesh.shape["row"], 4, 4, 4), ("row", "col_0", "col_1", "col_2")
    )
    placed = (P(COL, None), P(COL, "row"), P(COL, "row"))
    return jax.shard_map(
        per_device,
        mesh=torus,
        in_specs=placed,
        out_specs=(P(COL, "row"), P(COL, "row")),
        check_vma=False,
    )
```

profile of v0, /device:TPU:1, one launch (start us, length us, event | category | flops | bytes accessed | tf_op | source)
XLA Modules:
  0.0 517.6 jit_solution(3365251138714423770)
XLA Ops:
  8.0 0.0 copy-start
  8.0 0.0 reduce-scatter.5.cloned.1.call-start
  8.1 1.1 copy-done
  9.1 10.0 %convolution_multiply_fusion = f32[4096,1024]{1,0:T(8,128)} fusion(bf16[384,1024]{1,0:T(8,128)(2,1)S(1)} %copy-done, bf16[384,4096]{1,0:T(8,128)(2,1)} %param.3), kind=kOutput, calls=%fused_computation | convolution fusion | flops 3226992640 | bytes 20709376 | tf_op jit(solution)/shard_map/dot_general | solution.py:28
  19.2 0.0 reduce-scatter.5.cloned.1.call-update
  19.2 0.0 all-gather.2.cloned.1.call-start
  19.2 0.5 all-gather.2.cloned.1.call-update
  19.8 0.0 reduce-scatter.7.cloned.1.call-start
  19.8 153.7 %reduce-scatter.5.cloned.1.call-done = f32[1024,1024]{1,0:T(8,128)} async-done(((f32[4096,1024]{1,0:T(8,128)}), f32[1024,1024]{1,0:T(8,128)}) %reduce-scatter.5.cloned.1.call-update) | async-done | bytes 4194320 | tf_op jit(solution)/shard_map/reduce_scatter | solution.py:12
  173.5 0.0 reduce-scatter.7.cloned.1.call-update
  173.6 0.0 reduce-scatter.11.cloned.1.call-start
  173.6 186.3 %all-gather.2.cloned.1.call-done = bf16[4096,1024]{1,0:T(8,128)(2,1)} async-done(((bf16[64,1024]{1,0:T(8,128)(2,1)}), bf16[4096,1024]{1,0:T(8,128)(2,1)}) %all-gather.2.cloned.1.call-update) | async-done | bytes 8388624 | tf_op jit(solution)/shard_map/all_gather | solution.py:24
  359.9 10.3 %convolution_convert_fusion = bf16[384,4096]{1,0:T(8,128)(2,1)} fusion(bf16[384,1024]{1,0:T(8,128)(2,1)S(1)} %copy-done, bf16[4096,1024]{1,0:T(8,128)(2,1)} %all-gather.2.cloned.1.call-done), kind=kOutput, calls=%fused_computation.1 | convolution fusion | flops 3222798336 | bytes 12320768 | tf_op jit(solution)/shard_map/dot_general | solution.py:22
  370.3 0.0 reduce-scatter.11.cloned.1.call-update
  370.3 0.0 reduce-scatter.9.cloned.1.call-start
  370.3 0.0 reduce-scatter.7.cloned.1.call-done
  370.4 0.5 reduce-scatter.9.cloned.1.call-update
  370.9 108.1 %reduce-scatter.11.cloned.1.call-done = bf16[384,1024]{1,0:T(8,128)(2,1)} async-done(((bf16[384,4096]{1,0:T(8,128)(2,1)}), bf16[384,1024]{1,0:T(8,128)(2,1)}) %reduce-scatter.11.cloned.1.call-update) | async-done | bytes 786448 | tf_op jit(solution)/shard_map/reduce_scatter | solution.py:32
  479.0 2.5 select_convert_fusion
  481.5 28.9 %reduce-scatter.9.cloned.1.call-done = f32[64,1024]{1,0:T(8,128)} async-done(((f32[256,1024]{1,0:T(8,128)}), f32[64,1024]{1,0:T(8,128)}) %reduce-scatter.9.cloned.1.call-update) | async-done | bytes 262160 | tf_op jit(solution)/shard_map/reduce_scatter | solution.py:12
Async XLA Ops:
  8.0 1.1 copy-start
  8.0 165.5 %reduce-scatter.5.cloned.1.call-start = ((), (), s32[]{:S(2)}) async-start(), calls=%async_computation.4 | async-start | bytes 20971520 | tf_op jit(solution)/shard_map/reduce_scatter | solution.py:12
  19.2 340.7 %all-gather.2.cloned.1.call-start = ((), (), s32[]{:S(2)}) async-start(), calls=%async_computation.7 | async-start | bytes 8519680 | tf_op jit(solution)/shard_map/all_gather | solution.py:24
  19.8 350.6 %reduce-scatter.7.cloned.1.call-start = ((), (), s32[]{:S(2)}) async-start(), calls=%async_computation.5 | async-start | bytes 5242880 | tf_op jit(solution)/shard_map/reduce_scatter | solution.py:12
  173.6 305.4 %reduce-scatter.11.cloned.1.call-start = ((), (), s32[]{:S(2)}) async-start(), calls=%async_computation.8 | async-start | bytes 3932160 | tf_op jit(solution)/shard_map/reduce_scatter | solution.py:32
  370.3 140.2 %reduce-scatter.9.cloned.1.call-start = ((), (), s32[]{:S(2)}) async-start(), calls=%async_computation.6 | async-start | bytes 1310720 | tf_op jit(solution)/shard_map/reduce_scatter | solution.py:12
Sparse Core Ops, SparseCore 0:
  19.3 154.1 reduce-scatter.4
  176.1 113.8 reduce-scatter.6
  370.4 108.5 reduce-scatter.10
  482.0 28.4 reduce-scatter.8
Sparse Core Ops, SparseCore 1:
  21.5 338.4 all-gather.1
where the time goes:
time: 518 us
  waiting for transfers between devices  478 us (92%)
  matrix products  20.4 us (4%)
  between operations  15.2 us (3%)
    all_gather x1, waiting for transfers between devices, per_device(): lax.all_gather(w_down, COL, axis=0, tiled=True)  186 us
    reduce_scatter x3, waiting for transfers between devices, summed_rows(): subtotal = lax.psum_scatter(subtotal, axis, scatter_dimension=0, tiled=True)  183 us
    reduce_scatter x1, waiting for transfers between devices, per_device(): lax.psum_scatter(partial_sum.astype(jnp.bfloat16), 'row', scatter_dimensi...  108 us
  transfers between devices with their start and end apart: 5, of which 4 were waited for; matrix products, arithmetic and copies ran while one was open for 2% of the time, Pallas kernels for 0%

commit v1 on v0

--- a/solution.py
+++ b/solution.py
@@ -5,6 +5,11 @@
 from jax.sharding import PartitionSpec as P
 
 COL = ("col_0", "col_1", "col_2")
+
+
+def all_by_exchange(array, mesh_axis, d):
+    sent = jnp.stack([array] * lax.axis_size(mesh_axis))
+    return jnp.concatenate(lax.all_to_all(sent, mesh_axis, 0, 0), axis=d)
 
 
 def summed_rows(subtotal, axes):
@@ -21,7 +26,7 @@
     quarter = hidden.shape[1] // row_count
     partial_sum = lax.dot_general(
         grad_out,
-        lax.all_gather(w_down, COL, axis=0, tiled=True),
+        all_by_exchange(w_down, COL, 0),
         (((1,), (1,)), ((), ())),
         preferred_element_type=jnp.float32,
     )

time: 518 us -> 436 us (0.84)
  waiting for transfers between devices: 478 us -> 380 us
  starting transfers between devices: 0.2 us -> 13 us
    all_gather x1 -> x0, waiting for transfers between devices: 186 us -> none  [per_device(): lax.all_gather(w_down, COL, axis=0, tiled=True)]
    reduce_scatter x3, waiting for transfers between devices: 183 us -> 308 us  [summed_rows(): subtotal = lax.psum_scatter(subtotal, axis, scatter_dimension=0, tiled=True)]
    reduce_scatter x1, waiting for transfers between devices: 108 us -> 72 us  [per_device(): lax.psum_scatter(partial_sum.astype(jnp.bfloat16), 'row', scatter_dimensi...]
    all_to_all x0 -> x1, starting transfers between devices: none -> 12.8 us  [all_by_exchange(): return jnp.concatenate(lax.all_to_all(sent, mesh_axis, 0, 0), axis=d)]
  transfers between devices with their start and end apart: 5 -> 5, of which waited for: 4 -> 4; matrix products, arithmetic and copies ran while one was open for 2% -> 4% of each run, Pallas kernels for 0% -> 0%
where the time goes in v1:
time: 436 us; the launch traced here: 435 us
  waiting for transfers between devices  380 us (87%)
  matrix products  20.4 us (5%)
  between operations  13.8 us (3%)
  starting transfers between devices  13 us (3%)
  local copies, waits for them, and re-layouts  6.24 us (1%)
    reduce_scatter x3, waiting for transfers between devices, summed_rows(): subtotal = lax.psum_scatter(subtotal, axis, scatter_dimension=0, tiled=True)  308 us
    reduce_scatter x1, waiting for transfers between devices, per_device(): lax.psum_scatter(partial_sum.astype(jnp.bfloat16), 'row', scatter_dimensi...  72 us
    all_to_all x1, starting transfers between devices, all_by_exchange(): return jnp.concatenate(lax.all_to_all(sent, mesh_axis, 0, 0), axis=d)  12.8 us
    dot_general x1, matrix products, per_device(): lax.dot_general(grad_out, all_by_exchange(w_down, COL, 0), (((1,), (1,)),...  10.3 us
    dot_general x1, matrix products, per_device(): lax.dot_general(hidden, grad_out, (((0,), (0,)), ((), ())), preferred_ele...  10 us
  transfers between devices with their start and end apart: 5, of which 4 were waited for; matrix products, arithmetic and copies ran while one was open for 4% of the time, Pallas kernels for 0%

profile of v1, /device:TPU:1, one launch (start us, length us, event | category | flops | bytes accessed | tf_op | source)
XLA Modules:
  0.0 435.4 jit_solution(3062430325637846897)
XLA Ops:
  7.2 0.0 copy-start
  7.2 0.0 reduce-scatter.5.cloned.1.call-start
  7.2 1.1 copy-done
  8.3 10.0 %convolution_multiply_fusion = f32[4096,1024]{1,0:T(8,128)} fusion(bf16[384,1024]{1,0:T(8,128)(2,1)S(1)} %copy-done, bf16[384,4096]{1,0:T(8,128)(2,1)} %param.3), kind=kOutput, calls=%fused_computation | convolution fusion | flops 3226992640 | bytes 20709376 | tf_op jit(solution)/shard_map/dot_general | solution.py:33
  18.3 0.0 copy-start.1
  18.3 0.0 reduce-scatter.5.cloned.1.call-update
  18.4 0.9 copy-done.1
  19.2 4.3 stack.2
  23.5 12.8 %all-to-all-start = ((bf16[64,64,1024]{2,1,0:T(8,128)(2,1)}), bf16[64,64,1024]{2,1,0:T(8,128)(2,1)}, u32[]{:S(2)}, u32[]{:S(2)}) async-start(bf16[64,64,1024]{2,1,0:T(8,128)(2,1)} %stack.2), calls=%async_computation.3 | async-start | bytes 16777216 | tf_op jit(solution)/shard_map/all_to_all | solution.py:12
  36.3 0.0 reduce-scatter.7.cloned.1.call-start
  36.4 226.3 %reduce-scatter.5.cloned.1.call-done = f32[1024,1024]{1,0:T(8,128)} async-done(((f32[4096,1024]{1,0:T(8,128)}), f32[1024,1024]{1,0:T(8,128)}) %reduce-scatter.5.cloned.1.call-update) | async-done | bytes 4194320 | tf_op jit(solution)/shard_map/reduce_scatter | solution.py:17
  262.7 0.0 reduce-scatter.7.cloned.1.call-update
  262.7 0.0 reduce-scatter.11.cloned.1.call-start
  262.8 0.0 all-to-all-done
  262.8 10.3 %convolution_convert_fusion = bf16[384,4096]{1,0:T(8,128)(2,1)} fusion(bf16[384,1024]{1,0:T(8,128)(2,1)S(1)} %copy-done, bf16[4096,1024]{1,0:T(8,128)(2,1)} %bitcast), kind=kOutput, calls=%fused_computation.1 | convolution fusion | flops 3222798336 | bytes 12320768 | tf_op jit(solution)/shard_map/dot_general | solution.py:27
  273.1 0.0 reduce-scatter.11.cloned.1.call-update
  273.2 0.0 reduce-scatter.9.cloned.1.call-start
  273.2 52.3 %reduce-scatter.7.cloned.1.call-done = f32[256,1024]{1,0:T(8,128)} async-done(((f32[1024,1024]{1,0:T(8,128)}), f32[256,1024]{1,0:T(8,128)}) %reduce-scatter.7.cloned.1.call-update) | async-done | bytes 1048592 | tf_op jit(solution)/shard_map/reduce_scatter | solution.py:17
  325.5 0.0 reduce-scatter.9.cloned.1.call-update
  325.5 72.0 %reduce-scatter.11.cloned.1.call-done = bf16[384,1024]{1,0:T(8,128)(2,1)} async-done(((bf16[384,4096]{1,0:T(8,128)(2,1)}), bf16[384,1024]{1,0:T(8,128)(2,1)}) %reduce-scatter.11.cloned.1.call-update) | async-done | bytes 786448 | tf_op jit(solution)/shard_map/reduce_scatter | solution.py:37
  397.4 2.5 select_convert_fusion
  400.0 28.9 %reduce-scatter.9.cloned.1.call-done = f32[64,1024]{1,0:T(8,128)} async-done(((f32[256,1024]{1,0:T(8,128)}), f32[64,1024]{1,0:T(8,128)}) %reduce-scatter.9.cloned.1.call-update) | async-done | bytes 262160 | tf_op jit(solution)/shard_map/reduce_scatter | solution.py:17
Async XLA Ops:
  7.2 1.1 copy-start
  7.2 255.5 %reduce-scatter.5.cloned.1.call-start = ((), (), s32[]{:S(2)}) async-start(), calls=%async_computation.5 | async-start | bytes 20971520 | tf_op jit(solution)/shard_map/reduce_scatter | solution.py:17
  18.3 0.9 copy-start.1
  23.5 239.3 %all-to-all-start = ((bf16[64,64,1024]{2,1,0:T(8,128)(2,1)}), bf16[64,64,1024]{2,1,0:T(8,128)(2,1)}, u32[]{:S(2)}, u32[]{:S(2)}) async-start(bf16[64,64,1024]{2,1,0:T(8,128)(2,1)} %stack.2), calls=%async_computation.3 | async-start | bytes 16777216 | tf_op jit(solution)/shard_map/all_to_all | solution.py:12
  36.3 289.1 %reduce-scatter.7.cloned.1.call-start = ((), (), s32[]{:S(2)}) async-start(), calls=%async_computation.6 | async-start | bytes 5242880 | tf_op jit(solution)/shard_map/reduce_scatter | solution.py:17
  262.7 134.7 %reduce-scatter.11.cloned.1.call-start = ((), (), s32[]{:S(2)}) async-start(), calls=%async_computation.8 | async-start | bytes 3932160 | tf_op jit(solution)/shard_map/reduce_scatter | solution.py:37
  273.2 155.8 %reduce-scatter.9.cloned.1.call-start = ((), (), s32[]{:S(2)}) async-start(), calls=%async_computation.7 | async-start | bytes 1310720 | tf_op jit(solution)/shard_map/reduce_scatter | solution.py:17
Sparse Core Ops, SparseCore 0:
  18.5 244.1 reduce-scatter.4
  265.3 60.1 reduce-scatter.6
  328.2 69.1 reduce-scatter.10
  400.4 28.4 reduce-scatter.8
